TPU v7x, 256 devices: a whole 4x4x8 slice. The times are simulated.
256 devices in a mesh: row: 8 (over y, core), col: 32 (over x, z).
Axes of the slice: x: 4, y: 4, z: 8, core: 2. Of those that a mesh axis runs over, the one named last changes fastest.
Arguments:
- normal: float32 [8, 8, 256, 2, 32, 256], P(None, 'row', None, None, 'col'), may hold values from -1.5 to 1.5
- panel_inverse: float32 [256, 256], replicated, as said below
- rhs: float32 [8, 8, 256, 512], P(None, 'row', None, 'col'), may hold values from -0.009765625 to 0.009765625
- shifts: float32 [4], replicated, may hold values from 16 to 128
Outputs:
- schur: float32 [8, 8, 256, 2, 32, 256], P(None, 'row', None, None, 'col')
- eliminated: float32 [8, 8, 256, 512], P(None, 'row', None, 'col')
- applied: float32 [8, 8, 256, 512], P(None, 'row', None, 'col')
Inputs may be any that keep to these rules, and one draw needn't show every extreme that they name: `panel_inverse`: lower triangular with positive diagonal entries.
All inputs are finite; a program needn't handle non-finite values.
Results may differ from a plain program's by a relative error of at most 0.000076.
Values sent between devices are 32-bit elements; how exact they have to be, the bound alone decides.
No kernel may reach another device: no remote copies, remote signals or barrier semaphores. Data moves between devices by JAX's collectives and lax.ppermute only.
A program may use at most 64 MiB of HBM per device.

v0:
```python
import jax
import jax.numpy as jnp
from jax import lax
from jax.sharding import Mesh
from jax.sharding import PartitionSpec as P

R = 128
COL = ("col_0", "col_1")


def from_root(array, axes, root):
    array = jnp.where(lax.axis_index(axes) == root, array, jnp.zeros_like(array))
    for axis in axes:
        array = lax.psum(array, axis)
    return array


def picked(array, axis, root):
    return lax.dynamic_index_in_dim(lax.all_gather(array, axis), root, 0, keepdims=False)


def copy_for_each(array, axis):
    copies = jnp.broadcast_to(array, (lax.axis_size(axis), *array.shape))
    return lax.all_to_all(copies, axis, split_axis=0, concat_axis=0, tiled=True)


def laid_out(blocks, dim):
    shape = list(blocks.shape[1:])
    shape[dim] *= blocks.shape[0]
    return jnp.moveaxis(blocks, 0, dim).reshape(shape)


def collect(array, axis, dim):
    blocks = copy_for_each(array, axis)
    return laid_out(blocks, dim)


def over_pieces(array, axis):
    blocks = lax.all_gather(array, axis)
    return blocks.sum(axis=0)


def pick_blocks(blocks, spacing, offset):
    grouped = blocks.reshape((blocks.shape[0] // spacing, spacing) + blocks.shape[1:])
    return lax.dynamic_index_in_dim(grouped, offset, 1, keepdims=False)


def shards(normal, panel_inverse, rhs, shifts):
    high = lax.Precision.HIGHEST
    row_index = lax.axis_index("row")
    col_index = lax.axis_index(COL)
    nrow = lax.axis_size("row")
    ncol = lax.axis_size(COL)
    spacing = ncol // nrow
    brows, nb, bcols = (normal.shape[0], normal.shape[2], normal.shape[3])
    narrow = rhs.shape[3]
    wide = narrow * ncol
    tile = normal.reshape(brows * nb, bcols * nb)
    owner = col_index % nrow
    offset = col_index // nrow
    early = lax.all_gather(rhs.reshape(brows, nb, narrow), COL, axis=2, tiled=True)
    local_panel = jnp.dot(
        tile[:, :nb], panel_inverse.T, precision=high, preferred_element_type=jnp.float32
    )
    panel = from_root(local_panel, COL, 0)
    chosen = pick_blocks(panel.reshape(brows, nb, nb), spacing, offset)
    crossed = picked(chosen, "row", owner).reshape(bcols * nb, nb)
    updated = tile - jnp.dot(panel, crossed.T, precision=high, preferred_element_type=jnp.float32)
    leading = picked(rhs[0, 0], "row", 0)
    first = jnp.dot(panel_inverse, leading, precision=high, preferred_element_type=jnp.float32)
    reduced = rhs.reshape(brows * nb, narrow) - jnp.dot(
        panel, first, precision=high, preferred_element_type=jnp.float32
    )
    reduced = reduced.reshape(brows, nb, narrow)
    reduced = reduced.at[0].set(jnp.where(row_index == 0, first, reduced[0]))
    first_all = collect(first, COL, 1)
    spread = early.reshape(brows * nb, wide) - jnp.dot(
        panel, first_all, precision=high, preferred_element_type=jnp.float32
    )
    spread = spread.reshape(brows, nb, wide)
    spread = spread.at[0].set(jnp.where(row_index == 0, first_all, spread[0]))
    scales = lax.dynamic_slice_in_dim(jnp.repeat(shifts, R), col_index * narrow, narrow)
    partial_value = lax.dot_general(
        updated,
        spread.reshape(brows * nb, wide),
        (((0,), (0,)), ((), ())),
        precision=high,
        preferred_element_type=jnp.float32,
    )
    totals = over_pieces(partial_value, "row")
    totals = totals.reshape(bcols, nb, ncol, narrow)
    arrived = lax.all_to_all(totals, COL, split_axis=2, concat_axis=2, tiled=True)
    arrived = arrived.reshape(bcols, nb, spacing, nrow, narrow)
    arrived = lax.dynamic_index_in_dim(arrived, row_index, 3, keepdims=False)
    product = jnp.transpose(arrived, (0, 2, 1, 3)).reshape(brows, nb, narrow)
    applied = product + reduced * scales[None, None, :]
    schur = updated.reshape(brows, 1, nb, bcols, 1, nb)
    return (schur, reduced.reshape(brows, 1, nb, narrow), applied.reshape(brows, 1, nb, narrow))


def solution(mesh):
    split = Mesh(mesh.devices.reshape(mesh.shape["row"], 4, 8), ("row", "col_0", "col_1"))
    placed = (P(None, "row", None, None, COL, None), P(), P(None, "row", None, COL), P())
    return jax.shard_map(
        shards,
        mesh=split,
        in_specs=placed,
        out_specs=(
            P(None, "row", None, None, COL, None),
            P(None, "row", None, COL),
            P(None, "row", None, COL),
        ),
        check_vma=False,
    )
```

profile of v0, /device:TPU:32, one launch (start us, length us, event | category | flops | bytes accessed | tf_op | source)
XLA Modules:
  0.0 382.1 jit_solution(8864626879516154711)
XLA Ops:
  8.0 0.0 copy-start
  8.0 0.0 all-reduce.3.cloned.1.call-start
  8.1 15.9 %reduce.4 = f32[8,256,2,256]{3,2,1,0:T(2,128)} reduce(f32[8,1,256,2,1,256]{5,4,3,2,1,0:T(1,128)} %param.8, f32[]{:T(128)} %constant.112), dimensions={1,4}, to_apply=%param.8.reduce_sub_computation | reduce | bytes 8388612 | tf_op args[0]
  24.0 4.6 %copy.26 = f32[256,8,2,256]{3,1,2,0:T(8,128)} copy(f32[256,8,2,256]{3,2,1,0:T(2,128)} %bitcast.62) | data formatting | bytes 8388608
  28.5 0.0 copy-done
  28.5 0.0 copy-start.3
  28.5 4.8 %convolution_select_fusion = f32[2048,256]{1,0:T(8,128)} fusion(f32[256,256]{1,0:T(8,128)S(1)} %copy-done, f32[2048,512]{1,0:T(8,128)} %bitcast.58, pred[]{:T(512)S(6)} %eq.9), kind=kOutput, calls=%fused_computation.2 | convolution fusion | flops 1611137024 | bytes 4456449 | tf_op jit(solution)/shard_map/dot_general | solution.py:62
  33.3 0.0 all-reduce.3.cloned.1.call-update
  33.3 0.0 all-reduce.5.cloned.1.call-start
  33.4 66.4 %all-reduce.3.cloned.1.call-done = f32[2048,256]{1,0:T(8,128)} async-done(((f32[2048,256]{1,0:T(8,128)}), f32[2048,256]{1,0:T(8,128)}) %all-reduce.3.cloned.1.call-update) | async-done | bytes 2097168 | tf_op jit(solution)/shard_map/psum | solution.py:14
  99.8 0.0 all-reduce.5.cloned.1.call-update
  99.9 0.0 all-gather.10.cloned.1.call-start
  99.9 0.5 all-gather.10.cloned.1.call-update
  100.4 0.0 all-gather.8.cloned.1.call-start
  100.5 95.7 %all-reduce.5.cloned.1.call-done = f32[2048,256]{1,0:T(8,128)} async-done(((f32[2048,256]{1,0:T(8,128)}), f32[2048,256]{1,0:T(8,128)}) %all-reduce.5.cloned.1.call-update) | async-done | bytes 2097168 | tf_op jit(solution)/shard_map/psum | solution.py:14
  196.3 1.9 constant_dynamic-slice_fusion.2
  198.1 0.0 all-gather.8.cloned.1.call-update
  198.1 0.0 copy-done.3
  198.2 13.1 %all-gather.1 = f32[8,1,256,16]{2,3,1,0:T(8,128)S(1)} all-gather(f32[1,1,256,16]{2,3,1,0:T(8,128)S(1)} %slice.56), channel_id=3, replica_groups=mesh['row'=8,'col_0'=4,'col_1'=8] {'row'}, dimensions={0}, use_global_device_ids=true | all-gather | bytes 147456 | tf_op jit(solution)/shard_map/all_gather | solution.py:19
  211.3 0.3 fusion.5
  211.5 0.9 broadcast_in_dim.11
  212.4 9.2 %all-to-all-start = ((f32[32,256,16]{1,2,0:T(8,128)}), f32[32,256,16]{1,2,0:T(8,128)S(1)}, u32[]{:S(2)}, u32[]{:S(2)}) async-start(f32[32,256,16]{1,2,0:T(8,128)} %broadcast_in_dim.11), calls=%async_computation | async-start | bytes 1048576 | tf_op jit(solution)/shard_map/all_to_all | solution.py:24
  221.6 0.2 all-gather.12.cloned.1.call-start
  221.9 17.9 %all-to-all-done = f32[32,256,16]{1,2,0:T(8,128)S(1)} async-done(((f32[32,256,16]{1,2,0:T(8,128)}), f32[32,256,16]{1,2,0:T(8,128)S(1)}, u32[]{:S(2)}, u32[]{:S(2)}) %all-to-all-start) | async-done | bytes 524320 | tf_op jit(solution)/shard_map/all_to_all | solution.py:24
  239.7 0.2 copy.21
  239.9 0.0 copy-start.2
  239.9 0.0 all-gather.10.cloned.1.call-done
  240.0 5.5 %copy.20 = f32[8,1,256,512]{3,2,0,1:T(8,128)} copy(f32[8,1,256,512]{2,3,1,0:T(8,128)} %all-gather.10.cloned.1.call-done) | data formatting | bytes 8388608 | tf_op jit(solution)/shard_map/all_gather | solution.py:61
  245.5 0.0 copy-done.2
  245.5 5.3 %bitcast_subtract_fusion = f32[2048,512]{1,0:T(8,128)S(1)} fusion(f32[8,1,256,512]{3,2,0,1:T(8,128)} %copy.20, f32[2048,256]{1,0:T(8,128)S(1)} %copy-done.2, f32[256,512]{0,1:T(8,128)S(1)} %bitcast.65), kind=kOutput, calls=%fused_computation | convolution fusion | flops 3222274048 | bytes 11010048 | tf_op jit(solution)/shard_map/dot_general | solution.py:77
  250.8 2.0 copy.34
  252.8 0.9 fusion.2
  253.7 0.0 all-gather.8.cloned.1.call-done
  253.7 1.1 constant_dynamic-slice_fusion.1
  254.8 5.5 %convolution_subtract_fusion = f32[2048,512]{1,0:T(8,128)S(1)} fusion(f32[2048,512]{1,0:T(8,128)} %bitcast.59, f32[2048,256]{1,0:T(8,128)S(1)} %copy-done.2, f32[512,256]{1,0:T(8,128)S(1)} %bitcast.66), kind=kOutput, calls=%fused_computation.1 | convolution fusion | flops 3222274048 | bytes 11010048 | tf_op jit(solution)/shard_map/dot_general | solution.py:68
  260.3 0.0 copy-start.1
  260.3 1.9 copy-done.1
  262.2 16.2 %fusion.6 = f32[512,512]{1,0:T(8,128)} fusion(f32[2048,512]{1,0:T(8,128)S(1)} %convolution_subtract_fusion, f32[2048,512]{1,0:T(8,128)} %bitcast.12), kind=kOutput, calls=%fused_computation.19 | convolution fusion | flops 6442450944 | bytes 9437184 | tf_op jit(solution)/shard_map/dot_general | solution.py:83
  278.5 0.0 all-gather.12.cloned.1.call-update
  278.5 47.7 %all-gather.12.cloned.1.call-done = f32[4096,512]{1,0:T(8,128)} async-done(((f32[512,512]{1,0:T(8,128)}), f32[4096,512]{1,0:T(8,128)}) %all-gather.12.cloned.1.call-update) | async-done | bytes 8388624 | tf_op jit(solution)/shard_map/all_gather | solution.py:39
  326.1 4.5 %reduce_sum.9 = f32[512,512]{1,0:T(8,128)S(1)} reduce(f32[8,512,512]{2,1,0:T(8,128)} %bitcast.63, f32[]{:T(128)} %constant.101.clone.1), dimensions={0}, to_apply=%region_2.3 | reduce | flops 1835008 | bytes 9437188 | tf_op jit(solution)/shard_map/reduce_sum | solution.py:40
  330.6 1.3 copy.22
  331.9 2.8 reshape.136
  334.8 10.1 %all-to-all-start.1 = ((f32[2,256,32,16]{1,0,3,2:T(2,128)}), f32[2,256,32,16]{1,0,3,2:T(2,128)S(1)}, u32[]{:S(2)}, u32[]{:S(2)}) async-start(f32[2,256,32,16]{1,0,3,2:T(2,128)} %reshape.136), calls=%async_computation.1 | async-start | bytes 2097152 | tf_op jit(solution)/shard_map/all_to_all | solution.py:92
  344.9 0.7 copy.27
  345.5 0.7 broadcast_bitcast_fusion
  346.2 0.1 dynamic_slice.23
  346.3 2.8 convolution_subtract_fusion.1
  349.1 0.0 copy-start.4
  349.1 7.7 %reshape.148 = f32[8,1,256,2,1,256]{5,4,3,2,1,0:T(1,128)} reshape(f32[2048,512]{1,0:T(8,128)} %copy-done.1) | data formatting | bytes 8388608 | tf_op jit(solution)/shard_map/reshape | solution.py:97
  356.8 16.8 %all-to-all-done.1 = f32[2,256,32,16]{1,0,3,2:T(2,128)S(1)} async-done(((f32[2,256,32,16]{1,0,3,2:T(2,128)}), f32[2,256,32,16]{1,0,3,2:T(2,128)S(1)}, u32[]{:S(2)}, u32[]{:S(2)}) %all-to-all-start.1) | async-done | bytes 1048608 | tf_op jit(solution)/shard_map/all_to_all | solution.py:92
  373.6 0.1 copy.23
  373.8 0.0 copy-done.4
  373.8 0.7 bitcast_add_fusion
  (4 shorter events, 0.0 us)
Async XLA Ops:
  8.0 20.5 %copy-start = (f32[256,256]{1,0:T(8,128)S(1)}, f32[256,256]{1,0:T(8,128)}, u32[]{:S(2)}) copy-start(f32[256,256]{1,0:T(8,128)} %param.9) | copy-start | bytes 786436
  8.0 91.8 %all-reduce.3.cloned.1.call-start = ((), (), s32[]{:S(2)}) async-start(), calls=%async_computation.2 | async-start | bytes 4194304 | tf_op jit(solution)/shard_map/psum | solution.py:14
  28.5 169.6 %copy-start.3 = (f32[8,1,256,16]{2,3,1,0:T(8,128)S(1)}, f32[8,1,256,16]{2,3,1,0:T(8,128)}, u32[]{:S(2)}) copy-start(f32[8,1,256,16]{2,3,1,0:T(8,128)} %param.10) | copy-start | bytes 393220
  33.3 162.9 %all-reduce.5.cloned.1.call-start = ((), (), s32[]{:S(2)}) async-start(), calls=%async_computation.3 | async-start | bytes 4194304 | tf_op jit(solution)/shard_map/psum | solution.py:14
  99.9 140.1 %all-gather.10.cloned.1.call-start = ((), (), s32[]{:S(2)}) async-start(), calls=%async_computation.5 | async-start | bytes 4325376 | tf_op jit(solution)/shard_map/all_gather | solution.py:61
  100.4 153.2 %all-gather.8.cloned.1.call-start = ((), (), s32[]{:S(2)}) async-start(), calls=%async_computation.4 | async-start | bytes 4718592 | tf_op jit(solution)/shard_map/all_gather | solution.py:19
  212.4 27.3 %all-to-all-start = ((f32[32,256,16]{1,2,0:T(8,128)}), f32[32,256,16]{1,2,0:T(8,128)S(1)}, u32[]{:S(2)}, u32[]{:S(2)}) async-start(f32[32,256,16]{1,2,0:T(8,128)} %broadcast_in_dim.11), calls=%async_computation | async-start | bytes 1048576 | tf_op jit(solution)/shard_map/all_to_all | solution.py:24
  221.6 104.5 %all-gather.12.cloned.1.call-start = ((), (), s32[]{:S(2)}) async-start(), calls=%async_computation.6 | async-start | bytes 9437184 | tf_op jit(solution)/shard_map/all_gather | solution.py:39
  239.9 5.5 %copy-start.2 = (f32[2048,256]{1,0:T(8,128)S(1)}, f32[2048,256]{1,0:T(8,128)}, u32[]{:S(2)}) copy-start(f32[2048,256]{1,0:T(8,128)} %all-reduce.5.cloned.1.call-done) | copy-start | bytes 6291460
  260.3 2.0 copy-start.1
  334.8 38.8 %all-to-all-start.1 = ((f32[2,256,32,16]{1,0,3,2:T(2,128)}), f32[2,256,32,16]{1,0,3,2:T(2,128)S(1)}, u32[]{:S(2)}, u32[]{:S(2)}) async-start(f32[2,256,32,16]{1,0,3,2:T(2,128)} %reshape.136), calls=%async_computation.1 | async-start | bytes 2097152 | tf_op jit(solution)/shard_map/all_to_all | solution.py:92
  349.1 24.6 %copy-start.4 = (f32[8,256,16]{1,2,0:T(8,128)}, f32[8,256,16]{1,2,0:T(8,128)S(1)}, u32[]{:S(2)}) copy-start(f32[8,256,16]{1,2,0:T(8,128)S(1)} %fusion.4) | copy-start | bytes 393220
Sparse Core Ops, SparseCore 0:
  33.5 66.3 all-reduce.2
  102.2 94.0 all-reduce.4
Sparse Core Ops, SparseCore 1:
  102.9 92.5 all-gather.9
  198.2 34.9 all-gather.7
  278.6 47.5 all-gather.11
where the time goes:
time: 383 us; the launch traced here: 382 us
  waiting for transfers between devices  245 us (64%)
  matrix products  34.9 us (9%)
  local copies, waits for them, and re-layouts  31.6 us (8%)
  other arithmetic  22 us (6%)
  starting transfers between devices  19.6 us (5%)
  between operations  15.9 us (4%)
  blocking collectives  13.1 us (3%)
    psum x2, waiting for transfers between devices, from_root(): array = lax.psum(array, axis)  162 us
    all_gather x1, waiting for transfers between devices, over_pieces(): blocks = lax.all_gather(array, axis)  47.7 us
    all_to_all x1, waiting for transfers between devices, copy_for_each(): return lax.all_to_all(copies, axis, split_axis=0, concat_axis=0, tiled=True)  17.9 us
    all_to_all x1, waiting for transfers between devices, shards(): lax.all_to_all(totals, COL, split_axis=2, concat_axis=2, tiled=True)  16.8 us
    dot_general x1, matrix products, shards(): lax.dot_general(updated, spread.reshape(brows * nb, wide), (((0,), (0,)),...  16.2 us
    unnamed x1, other arithmetic  15.9 us
    all_gather x1, blocking collectives, picked(): lax.all_gather(array, axis)  13.1 us
    all_to_all x1, starting transfers between devices, shards(): lax.all_to_all(totals, COL, split_axis=2, concat_axis=2, tiled=True)  10.1 us
  transfers between devices with their start and end apart: 7, of which 5 were waited for; matrix products, arithmetic and copies ran while one was open for 8% of the time, Pallas kernels for 0%

commit v1 on v0

--- a/solution.py
+++ b/solution.py
@@ -11,7 +11,7 @@
 def from_root(array, axes, root):
     array = jnp.where(lax.axis_index(axes) == root, array, jnp.zeros_like(array))
     for axis in axes:
-        array = lax.psum(array, axis)
+        array = jnp.sum(lax.all_gather(array, axis), axis=0)
     return array
 
 

time: 383 us -> 552 us (1.44)
  waiting for transfers between devices: 245 us -> 407 us
  other arithmetic: 22 us -> 34.7 us
    all_gather x0 -> x2, waiting for transfers between devices: none -> 260 us  [from_root(): array = jnp.sum(lax.all_gather(array, axis), axis=0)]
    psum x2 -> x0, waiting for transfers between devices: 162 us -> none  [from_root(): array = lax.psum(array, axis)]
    all_gather x1, waiting for transfers between devices: 0.03 us -> 37.2 us  [shards(): lax.all_gather(rhs.reshape(brows, nb, narrow), COL, axis=2, tiled=True)]
    all_gather x1, waiting for transfers between devices: 0.01 us -> 19.9 us  [picked(): lax.all_gather(array, axis)]
    reduce_sum x0 -> x2, other arithmetic: none -> 12.7 us  [from_root(): array = jnp.sum(lax.all_gather(array, axis), axis=0)]
  transfers between devices with their start and end apart: 7 -> 7, of which waited for: 5 -> 7; matrix products, arithmetic and copies ran while one was open for 8% -> 6% of each run, Pallas kernels for 0% -> 0%
where the time goes in v1:
time: 552 us; the launch traced here: 551 us
  waiting for transfers between devices  407 us (74%)
  other arithmetic  34.7 us (6%)
  matrix products  33.9 us (6%)
  local copies, waits for them, and re-layouts  29.1 us (5%)
  starting transfers between devices  19.6 us (4%)
  between operations  14 us (3%)
  blocking collectives  13.1 us (2%)
    all_gather x2, waiting for transfers between devices, from_root(): array = jnp.sum(lax.all_gather(array, axis), axis=0)  260 us
    all_gather x1, waiting for transfers between devices, over_pieces(): blocks = lax.all_gather(array, axis)  52.3 us
    all_gather x1, waiting for transfers between devices, shards(): lax.all_gather(rhs.reshape(brows, nb, narrow), COL, axis=2, tiled=True)  37.2 us
    all_gather x1, waiting for transfers between devices, picked(): lax.all_gather(array, axis)  19.9 us
    all_to_all x1, waiting for transfers between devices, shards(): lax.all_to_all(totals, COL, split_axis=2, concat_axis=2, tiled=True)  18.9 us
    all_to_all x1, waiting for transfers between devices, copy_for_each(): return lax.all_to_all(copies, axis, split_axis=0, concat_axis=0, tiled=True)  18.3 us
    dot_general x1, matrix products, shards(): lax.dot_general(updated, spread.reshape(brows * nb, wide), (((0,), (0,)),...  16.2 us
    unnamed x1, other arithmetic  15.9 us
  transfers between devices with their start and end apart: 7, of which 7 were waited for; matrix products, arithmetic and copies ran while one was open for 6% of the time, Pallas kernels for 0%

profile of v1, /device:TPU:32, one launch (start us, length us, event | category | flops | bytes accessed | tf_op | source)
XLA Modules:
  0.0 551.3 jit_solution(8926751303388959762)
XLA Ops:
  7.2 0.0 copy-start
  7.2 0.0 all-gather.12.cloned.1.call-start
  7.2 15.9 %reduce.4 = f32[8,256,2,256]{3,2,1,0:T(2,128)} reduce(f32[8,1,256,2,1,256]{5,4,3,2,1,0:T(1,128)} %param.8, f32[]{:T(128)} %constant.112), dimensions={1,4}, to_apply=%param.8.reduce_sub_computation | reduce | bytes 8388612 | tf_op args[0]
  23.1 4.6 copy.33
  27.7 0.0 copy-done
  27.7 4.7 convolution_select_fusion
  32.4 0.0 all-gather.12.cloned.1.call-update
  32.5 0.0 all-gather.14.cloned.1.call-start
  32.5 88.3 %all-gather.12.cloned.1.call-done = f32[8192,256]{1,0:T(8,128)} async-done(((f32[2048,256]{1,0:T(8,128)}), f32[8192,256]{1,0:T(8,128)}) %all-gather.12.cloned.1.call-update) | async-done | bytes 8388624 | tf_op jit(solution)/shard_map/all_gather | solution.py:14
  120.8 5.5 %reduce_sum.27 = f32[2048,256]{1,0:T(8,128)} reduce(f32[4,2048,256]{2,1,0:T(8,128)} %bitcast.67, f32[]{:T(128)} %constant.101.clone.1), dimensions={0}, to_apply=%region_0.1 | reduce | flops 1572864 | bytes 10485764 | tf_op jit(solution)/shard_map/reduce_sum | solution.py:14
  126.3 0.0 all-gather.14.cloned.1.call-update
  126.4 0.0 all-gather.18.cloned.1.call-start
  126.4 0.7 all-gather.18.cloned.1.call-update
  127.1 0.0 all-gather.16.cloned.1.call-start
  127.2 171.3 %all-gather.14.cloned.1.call-done = f32[16384,256]{1,0:T(8,128)} async-done(((f32[2048,256]{1,0:T(8,128)}), f32[16384,256]{1,0:T(8,128)}) %all-gather.14.cloned.1.call-update) | async-done | bytes 16777232 | tf_op jit(solution)/shard_map/all_gather | solution.py:14
  298.5 0.0 copy-start.3
  298.5 7.1 %reduce_sum.28 = f32[2048,256]{1,0:T(8,128)S(1)} reduce(f32[8,2048,256]{2,1,0:T(8,128)} %bitcast.64, f32[]{:T(128)} %constant.101.clone.1), dimensions={0}, to_apply=%region_1.2 | reduce | flops 3670016 | bytes 18874372 | tf_op jit(solution)/shard_map/reduce_sum | solution.py:14
  305.6 0.8 constant_dynamic-slice_fusion.2
  306.4 0.0 all-gather.16.cloned.1.call-update
  306.4 0.0 copy-done.3
  306.5 13.1 %all-gather.3 = f32[8,1,256,16]{2,3,1,0:T(8,128)S(1)} all-gather(f32[1,1,256,16]{2,3,1,0:T(8,128)S(1)} %slice.56), channel_id=5, replica_groups=mesh['row'=8,'col_0'=4,'col_1'=8] {'row'}, dimensions={0}, use_global_device_ids=true | all-gather | bytes 147456 | tf_op jit(solution)/shard_map/all_gather | solution.py:19
  319.6 0.3 fusion.5
  319.8 0.9 broadcast_in_dim.11
  320.7 9.2 %all-to-all-start = ((f32[32,256,16]{1,2,0:T(8,128)}), f32[32,256,16]{1,2,0:T(8,128)S(1)}, u32[]{:S(2)}, u32[]{:S(2)}) async-start(f32[32,256,16]{1,2,0:T(8,128)} %broadcast_in_dim.11), calls=%async_computation | async-start | bytes 1048576 | tf_op jit(solution)/shard_map/all_to_all | solution.py:24
  329.9 0.2 all-gather.20.cloned.1.call-start
  330.2 18.3 %all-to-all-done = f32[32,256,16]{1,2,0:T(8,128)S(1)} async-done(((f32[32,256,16]{1,2,0:T(8,128)}), f32[32,256,16]{1,2,0:T(8,128)S(1)}, u32[]{:S(2)}, u32[]{:S(2)}) %all-to-all-start) | async-done | bytes 524320 | tf_op jit(solution)/shard_map/all_to_all | solution.py:24
  348.4 0.2 copy.28
  348.6 37.2 %all-gather.18.cloned.1.call-done = f32[8,1,256,512]{2,3,1,0:T(8,128)} async-done(((f32[8,1,256,16]{2,3,1,0:T(8,128)}), f32[8,1,256,512]{2,3,1,0:T(8,128)}) %all-gather.18.cloned.1.call-update) | async-done | bytes 4194320 | tf_op jit(solution)/shard_map/all_gather | solution.py:61
  385.9 5.3 copy.27
  391.2 5.3 bitcast_subtract_fusion
  396.5 2.0 copy.39
  398.6 0.9 fusion.2
  399.4 19.9 %all-gather.16.cloned.1.call-done = f32[16,1,256,256]{3,2,1,0:T(8,128)} async-done(((f32[2,1,256,256]{3,2,1,0:T(8,128)}), f32[16,1,256,256]{3,2,1,0:T(8,128)}) %all-gather.16.cloned.1.call-update) | async-done | bytes 4194320 | tf_op jit(solution)/shard_map/all_gather | solution.py:19
  419.3 1.1 constant_dynamic-slice_fusion.1
  420.4 5.5 convolution_subtract_fusion
  425.9 0.0 copy-start.2
  425.9 2.0 copy-done.2
  427.8 16.2 %fusion.6 = f32[512,512]{1,0:T(8,128)} fusion(f32[2048,512]{1,0:T(8,128)S(1)} %convolution_subtract_fusion, f32[2048,512]{1,0:T(8,128)} %bitcast.14), kind=kOutput, calls=%fused_computation.19 | convolution fusion | flops 6442450944 | bytes 9437184 | tf_op jit(solution)/shard_map/dot_general | solution.py:83
  444.1 0.0 all-gather.20.cloned.1.call-update
  444.1 52.3 %all-gather.20.cloned.1.call-done = f32[4096,512]{1,0:T(8,128)} async-done(((f32[512,512]{1,0:T(8,128)}), f32[4096,512]{1,0:T(8,128)}) %all-gather.20.cloned.1.call-update) | async-done | bytes 8388624 | tf_op jit(solution)/shard_map/all_gather | solution.py:39
  496.4 4.5 reduce_sum.29
  500.9 0.0 copy-start.5
  500.9 1.3 copy.29
  502.2 2.8 reshape.136
  505.1 10.1 %all-to-all-start.1 = ((f32[2,256,32,16]{1,0,3,2:T(2,128)}), f32[2,256,32,16]{1,0,3,2:T(2,128)S(1)}, u32[]{:S(2)}, u32[]{:S(2)}) async-start(f32[2,256,32,16]{1,0,3,2:T(2,128)} %reshape.136), calls=%async_computation.1 | async-start | bytes 2097152 | tf_op jit(solution)/shard_map/all_to_all | solution.py:92
  515.2 0.0 copy-done.5
  515.2 0.1 broadcast_bitcast_fusion
  515.2 0.1 dynamic_slice.23
  515.3 1.8 convolution_subtract_fusion.1
  517.2 0.0 copy-start.1
  517.2 0.0 copy-start.4
  517.2 7.7 %reshape.150 = f32[8,1,256,2,1,256]{5,4,3,2,1,0:T(1,128)} reshape(f32[2048,512]{1,0:T(8,128)} %copy-done.2) | data formatting | bytes 8388608 | tf_op jit(solution)/shard_map/reshape | solution.py:97
  525.0 18.9 %all-to-all-done.1 = f32[2,256,32,16]{1,0,3,2:T(2,128)S(1)} async-done(((f32[2,256,32,16]{1,0,3,2:T(2,128)}), f32[2,256,32,16]{1,0,3,2:T(2,128)S(1)}, u32[]{:S(2)}, u32[]{:S(2)}) %all-to-all-start.1) | async-done | bytes 1048608 | tf_op jit(solution)/shard_map/all_to_all | solution.py:92
  543.9 0.1 copy.30
  544.0 0.0 copy-done.4
  544.1 0.7 bitcast_add_fusion
  544.8 0.0 copy-done.1
  (5 shorter events, 0.0 us)
Async XLA Ops:
  7.2 20.5 %copy-start = (f32[256,256]{1,0:T(8,128)S(1)}, f32[256,256]{1,0:T(8,128)}, u32[]{:S(2)}) copy-start(f32[256,256]{1,0:T(8,128)} %param.9) | copy-start | bytes 786436
  7.2 113.6 %all-gather.12.cloned.1.call-start = ((), (), s32[]{:S(2)}) async-start(), calls=%async_computation.2 | async-start | bytes 10485760 | tf_op jit(solution)/shard_map/all_gather | solution.py:14
  32.5 266.0 %all-gather.14.cloned.1.call-start = ((), (), s32[]{:S(2)}) async-start(), calls=%async_computation.3 | async-start | bytes 18874368 | tf_op jit(solution)/shard_map/all_gather | solution.py:14
  126.4 259.5 %all-gather.18.cloned.1.call-start = ((), (), s32[]{:S(2)}) async-start(), calls=%async_computation.5 | async-start | bytes 4325376 | tf_op jit(solution)/shard_map/all_gather | solution.py:61
  127.1 292.2 %all-gather.16.cloned.1.call-start = ((), (), s32[]{:S(2)}) async-start(), calls=%async_computation.4 | async-start | bytes 4718592 | tf_op jit(solution)/shard_map/all_gather | solution.py:19
  298.5 8.0 %copy-start.3 = (f32[8,1,256,16]{2,3,1,0:T(8,128)S(1)}, f32[8,1,256,16]{2,3,1,0:T(8,128)}, u32[]{:S(2)}) copy-start(f32[8,1,256,16]{2,3,1,0:T(8,128)} %param.10) | copy-start | bytes 393220
  320.7 27.7 %all-to-all-start = ((f32[32,256,16]{1,2,0:T(8,128)}), f32[32,256,16]{1,2,0:T(8,128)S(1)}, u32[]{:S(2)}, u32[]{:S(2)}) async-start(f32[32,256,16]{1,2,0:T(8,128)} %broadcast_in_dim.11), calls=%async_computation | async-start | bytes 1048576 | tf_op jit(solution)/shard_map/all_to_all | solution.py:24
  329.9 166.5 %all-gather.20.cloned.1.call-start = ((), (), s32[]{:S(2)}) async-start(), calls=%async_computation.6 | async-start | bytes 9437184 | tf_op jit(solution)/shard_map/all_gather | solution.py:39
  425.9 2.0 copy-start.2
  500.9 14.2 %copy-start.5 = (f32[4]{0:T(128)S(1)}, f32[4]{0:T(128)}, u32[]{:S(2)}) copy-start(f32[4]{0:T(128)} %param.11) | copy-start | bytes 52
  505.1 38.8 %all-to-all-start.1 = ((f32[2,256,32,16]{1,0,3,2:T(2,128)}), f32[2,256,32,16]{1,0,3,2:T(2,128)S(1)}, u32[]{:S(2)}, u32[]{:S(2)}) async-start(f32[2,256,32,16]{1,0,3,2:T(2,128)} %reshape.136), calls=%async_computation.1 | async-start | bytes 2097152 | tf_op jit(solution)/shard_map/all_to_all | solution.py:92
  517.2 27.6 %copy-start.1 = (f32[256,256]{1,0:T(8,128)S(1)}, f32[256,256]{1,0:T(8,128)}, u32[]{:S(2)}) copy-start(f32[256,256]{1,0:T(8,128)} %param.9) | copy-start | bytes 786436
  517.2 26.8 %copy-start.4 = (f32[8,256,16]{1,2,0:T(8,128)}, f32[8,256,16]{1,2,0:T(8,128)S(1)}, u32[]{:S(2)}) copy-start(f32[8,256,16]{1,2,0:T(8,128)S(1)} %fusion.4) | copy-start | bytes 393220
Sparse Core Ops, SparseCore 0:
  32.6 88.1 all-gather.11
  126.5 171.9 all-gather.13
  301.0 84.7 all-gather.17
  387.6 31.6 all-gather.15
  444.2 52.1 all-gather.19
